TPU v7x, 512 devices: a whole 4x8x8 slice. The times are simulated.
512 devices in a mesh: dp: 64 (over z, y), tensor: 8 (over x, core).
Axes of the slice: x: 4, y: 8, z: 8, core: 2. Of those that a mesh axis runs over, the one named last changes fastest.
Arguments:
- tokens: bfloat16 [8192, 2048], P('dp'), may hold values from -8 to 8
- grad_out: bfloat16 [8192, 2048], P('dp'), may hold values from -6 to 6
- route_ids: int32 [8192, 4], P('dp'), may hold values from 0 to 59, as said below
- expert_map: int32 [60], replicated, may hold values from 0 to 63, as said below
- router: bfloat16 [2048, 60], replicated, may hold values from -1 to 1
- shared_gate: bfloat16 [2048], replicated, may hold values from -0.125 to 0.125
- sh_gate: bfloat16 [2048, 2816], P('dp', 'tensor'), may hold values from -0.125 to 0.125
- sh_up: bfloat16 [2048, 2816], P('dp', 'tensor'), may hold values from -0.125 to 0.125
- sh_down: bfloat16 [2816, 2048], P('tensor', 'dp'), may hold values from -0.109375 to 0.109375
- ex_gate: bfloat16 [64, 2048, 1408], P('dp', None, 'tensor'), may hold values from -0.125 to 0.125
- ex_up: bfloat16 [64, 2048, 1408], P('dp', None, 'tensor'), may hold values from -0.125 to 0.125
- ex_down: bfloat16 [64, 1408, 2048], P('dp', 'tensor'), may hold values from -0.15625 to 0.15625
Outputs:
- mixed: bfloat16 [8192, 2048], P('dp', 'tensor')
- grad_tokens: bfloat16 [8192, 2048], P('dp', 'tensor')
Inputs may be any that keep to these rules, and one draw needn't show every extreme that they name: `route_ids`: each row names 4 different experts. Within the rows of one device (aligned blocks of 128 rows), no expert is named more than 9 times over all 4 columns, and some expert is named exactly 9 times. Entries are distinct. Expert e uses the weights of slot expert_map[e]; slot s is held by index s // 1 of dp. Slots that no expert names are not used.
All inputs are finite; a program needn't handle non-finite values.
Results may differ from a plain program's by a relative error of at most 0.011.
Values may be sent and summed in bfloat16 or wider, within the bound.
A program may use at most 64 MiB of HBM per device.

v0:
```python
import jax
import jax.numpy as jnp
from jax import lax
from jax.sharding import PartitionSpec as P

CAP = 9


def turned_gather(arrays, axis, dims):
    turned = [jnp.moveaxis(a, dim, 0) for a, dim in zip(arrays, dims)]
    both = jnp.concatenate([t.reshape(len(t), -1) for t in turned], axis=1)
    result, at, outs = (lax.all_gather(both, axis, axis=0, tiled=True), 0, [])
    for t, dim in zip(turned, dims):
        share = result[:, at : at + t[0].size].reshape(-1, *t.shape[1:])
        outs.append(jnp.moveaxis(share, 0, dim))
        at += t[0].size
    return tuple(outs)


def in_one_piece(arrays, axis, split_dim, concat_dim, along):
    ends, at = ([], 0)
    for a in arrays[:-1]:
        at += a.shape[along]
        ends.append(at)
    both = jnp.concatenate(arrays, axis=along)
    return tuple(
        jnp.split(
            lax.all_to_all(both, axis, split_axis=split_dim, concat_axis=concat_dim, tiled=True),
            ends,
            axis=along,
        )
    )


def in_one_piece_2(arrays, axis, dim, along):
    ends, at = ([], 0)
    for a in arrays[:-1]:
        at += a.shape[along]
        ends.append(at)
    both = jnp.concatenate(arrays, axis=along)
    return tuple(jnp.split(lax.all_gather(both, axis, axis=dim, tiled=True), ends, axis=along))


def copy_for_each(x, axis):
    peers = lax.axis_size(axis)
    return lax.all_to_all(jnp.broadcast_to(x[None], (peers, *x.shape)), axis, 0, 0, tiled=True)


def of_everyone(x, axis):
    return copy_for_each(x, axis).sum(axis=0)


def together(arrays, axis):
    line, at, outs = (jnp.concatenate([a.reshape(-1) for a in arrays]), 0, [])
    subtotal = of_everyone(line, axis)
    for a in arrays:
        outs.append(subtotal[at : at + a.size].reshape(a.shape))
        at += a.size
    return tuple(outs)


def side_by_side(arrays, axis, dim, along):
    ends, at = ([], 0)
    for a in arrays[:-1]:
        at += a.shape[along]
        ends.append(at)
    both = jnp.concatenate(arrays, axis=along)
    return tuple(
        jnp.split(lax.psum_scatter(both, axis, scatter_dimension=dim, tiled=True), ends, axis=along)
    )


def silu_pair(pre_gate):
    sigmoid_val = 1.0 / (1.0 + jnp.exp(-pre_gate))
    return (pre_gate * sigmoid_val, sigmoid_val * (1.0 + pre_gate * (1.0 - sigmoid_val)))


def contract_last(left, right):
    return lax.dot_general(
        left, right, (((1,), (1,)), ((), ())), preferred_element_type=jnp.float32
    )


def expert_block(rows_in, rows_cot, w_gate, w_up, w_down):
    pre_gate = jnp.dot(rows_in, w_gate, preferred_element_type=jnp.float32)
    pre_up = jnp.dot(rows_in, w_up, preferred_element_type=jnp.float32)
    active, derivative = silu_pair(pre_gate)
    hidden = (active * pre_up).astype(jnp.bfloat16)
    result = jnp.dot(hidden, w_down, preferred_element_type=jnp.float32)
    grad_hidden = contract_last(rows_cot, w_down)
    grad_gate = (grad_hidden * pre_up * derivative).astype(jnp.bfloat16)
    grad_up = (grad_hidden * active).astype(jnp.bfloat16)
    backward = contract_last(grad_gate, w_gate) + contract_last(grad_up, w_up)
    return (result, backward)


def expert_batch(rows_in, rows_cot, w_gate, w_up, w_down):
    pre_gate = jnp.einsum("slcd,ldf->slcf", rows_in, w_gate, preferred_element_type=jnp.float32)
    pre_up = jnp.einsum("slcd,ldf->slcf", rows_in, w_up, preferred_element_type=jnp.float32)
    active, derivative = silu_pair(pre_gate)
    hidden = (active * pre_up).astype(jnp.bfloat16)
    result = jnp.einsum(
        "slcf,lfd->slcd", hidden, w_down, preferred_element_type=jnp.float32
    ).astype(jnp.bfloat16)
    grad_hidden = jnp.einsum("slcd,lfd->slcf", rows_cot, w_down, preferred_element_type=jnp.float32)
    grad_gate = (grad_hidden * pre_up * derivative).astype(jnp.bfloat16)
    grad_up = (grad_hidden * active).astype(jnp.bfloat16)
    grad_both = jnp.concatenate([grad_gate, grad_up], axis=3)
    weight_both = jnp.concatenate([w_gate, w_up], axis=2)
    backward = jnp.einsum(
        "slcf,ldf->slcd", grad_both, weight_both, preferred_element_type=jnp.float32
    )
    return (result, backward.astype(jnp.bfloat16))


def shards(
    tokens,
    grad_out,
    route_ids,
    expert_map,
    router,
    shared_gate,
    sh_gate,
    sh_up,
    sh_down,
    ex_gate,
    ex_up,
    ex_down,
):
    tok_dev, width = tokens.shape
    top_count = route_ids.shape[1]
    expert_count = router.shape[1]
    dp_size = lax.axis_size("dp")
    tensor_size = lax.axis_size("tensor")
    tensor_rank = lax.axis_index("tensor")
    local_slots = ex_gate.shape[0]
    col_width = width // tensor_size
    col_start = tensor_rank * col_width
    buffer_rows = dp_size * local_slots * CAP
    slot_rows = local_slots * CAP
    flat_ids = route_ids.reshape(-1)
    chosen = (flat_ids[:, None] == jnp.arange(expert_count, dtype=jnp.int32)[None, :]).astype(
        jnp.int32
    )
    earlier = jnp.sum((jnp.cumsum(chosen, axis=0) - chosen) * chosen, axis=1)
    slot_of = jnp.sum(chosen * expert_map[None, :], axis=1)
    position = slot_of * CAP + earlier
    token_index = jnp.arange(tok_dev * top_count, dtype=jnp.int32) // top_count
    source_rows = jnp.full((buffer_rows,), tok_dev, jnp.int32).at[position].set(token_index)

    def fetch_rows(table):
        padded = jnp.concatenate([table, jnp.zeros((1, table.shape[1]), table.dtype)], axis=0)
        return jnp.take(padded, source_rows, axis=0)

    def run_routed():
        part_in = lax.dynamic_slice_in_dim(tokens, col_start, col_width, 1)
        part_cot = lax.dynamic_slice_in_dim(grad_out, col_start, col_width, 1)
        send_in = fetch_rows(part_in).reshape(dp_size, slot_rows, col_width)
        send_cot = fetch_rows(part_cot).reshape(dp_size, slot_rows, col_width)
        got_in, got_cot = in_one_piece((send_in, send_cot), "dp", 0, 0, 1)
        got_in, got_cot = in_one_piece_2((got_in, got_cot), "tensor", 2, 0)
        grid_shape = (dp_size, local_slots, CAP, width)
        result, backward = expert_batch(
            got_in.reshape(grid_shape), got_cot.reshape(grid_shape), ex_gate, ex_up, ex_down
        )
        split_out = result.reshape(buffer_rows, tensor_size, col_width)
        split_back = backward.reshape(buffer_rows, tensor_size, col_width)
        met_out, met_back = in_one_piece((split_out, split_back), "tensor", 1, 1, 0)
        summed_out = jnp.sum(met_out.astype(jnp.float32), axis=1).reshape(
            dp_size, slot_rows, col_width
        )
        summed_back = jnp.sum(met_back.astype(jnp.float32), axis=1).reshape(
            dp_size, slot_rows, col_width
        )
        came_out, came_back = tuple(
            (
                part.astype(jnp.float32)
                for part in in_one_piece(
                    (summed_out.astype(jnp.bfloat16), summed_back.astype(jnp.bfloat16)),
                    "dp",
                    0,
                    0,
                    1,
                )
            )
        )
        return (came_out.reshape(buffer_rows, col_width), came_back.reshape(buffer_rows, col_width))

    routed_out, routed_back = run_routed()
    weights = turned_gather((sh_gate, sh_up, sh_down), "dp", (0, 0, 1))
    full_gate, full_up, full_down = weights
    sh_out, sh_back = expert_block(tokens, grad_out, full_gate, full_up, full_down)
    routed_width = routed_out.shape[1]
    expert_out = jnp.take(routed_out, position, axis=0).reshape(tok_dev, top_count, routed_width)
    expert_back = jnp.take(routed_back, position, axis=0).reshape(tok_dev, top_count, routed_width)
    logits = jnp.dot(tokens, router, preferred_element_type=jnp.float32)
    exp_logit = jnp.exp(logits)
    prob_table = exp_logit / jnp.sum(exp_logit, axis=1, keepdims=True)
    picked = chosen.reshape(tok_dev, top_count, expert_count).astype(jnp.float32)
    gate_weights = jnp.sum(picked * prob_table[:, None, :], axis=2)
    shared_scale = 1.0 / (
        1.0 + jnp.exp(-jnp.dot(tokens, shared_gate, preferred_element_type=jnp.float32))
    )
    shared_part = jnp.sum(grad_out.astype(jnp.float32) * sh_out, axis=1)
    cot_cols = lax.dynamic_slice_in_dim(grad_out, col_start, col_width, 1).astype(jnp.float32)
    dots_part = jnp.sum(cot_cols[:, None, :] * expert_out, axis=2)
    routed_mixed = jnp.sum(gate_weights[:, :, None] * expert_out, axis=1)
    routed_grad = jnp.sum(gate_weights[:, :, None] * expert_back, axis=1)
    mixed_part = shared_scale[:, None] * sh_out
    grad_part = shared_scale[:, None] * sh_back
    out_dots, shared_dots = together((dots_part, shared_part), "tensor")
    mixed_cols, grad_cols = tuple(
        (
            part.astype(jnp.float32)
            for part in side_by_side(
                (mixed_part.astype(jnp.bfloat16), grad_part.astype(jnp.bfloat16)), "tensor", 1, 0
            )
        )
    )
    mixed_cols = mixed_cols + routed_mixed
    grad_cols = grad_cols + routed_grad
    grad_prob = jnp.sum(picked * out_dots[:, :, None], axis=1)
    dlogits = prob_table * (grad_prob - jnp.sum(gate_weights * out_dots, axis=1, keepdims=True))
    router_cols = lax.dynamic_slice_in_dim(router, col_start, col_width, 0).astype(jnp.float32)
    grad_router = lax.dot_general(
        dlogits,
        router_cols,
        (((1,), (1,)), ((), ())),
        precision=lax.Precision.HIGHEST,
        preferred_element_type=jnp.float32,
    )
    gate_cols = lax.dynamic_slice_in_dim(shared_gate, col_start, col_width, 0).astype(jnp.float32)
    slope_term = shared_dots * shared_scale * (1.0 - shared_scale)
    grad_total = grad_cols + grad_router + slope_term[:, None] * gate_cols[None, :]
    return (mixed_cols.astype(jnp.bfloat16), grad_total.astype(jnp.bfloat16))


def solution(mesh):
    placed = (
        P("dp", None),
        P("dp", None),
        P("dp", None),
        P(),
        P(),
        P(),
        P("dp", "tensor"),
        P("dp", "tensor"),
        P("tensor", "dp"),
        P("dp", None, "tensor"),
        P("dp", None, "tensor"),
        P("dp", "tensor", None),
    )
    return jax.shard_map(
        shards,
        mesh=mesh,
        in_specs=placed,
        out_specs=(P("dp", "tensor"), P("dp", "tensor")),
        check_vma=False,
    )
```

profile of v0, /device:TPU:1, one launch (start us, length us, event | category | flops | bytes accessed | tf_op | source)
XLA Modules:
  0.0 265.0 jit_solution(9257027790201195252)
XLA Ops:
  7.2 0.8 copy.47
  8.3 1.2 reduce-window.6
  10.1 0.8 select_reduce_fusion
  10.8 2.4 scatter_custom_fusion
  13.3 0.9 constant_dynamic-slice_fusion
  14.3 2.7 %gather_fusion.1 = bf16[576,256]{1,0:T(8,128)(2,1)S(1)} fusion(bf16[129,256]{1,0:T(8,128)(2,1)S(1)} %concatenate.36, s32[1024]{0:T(1024)S(1)} %pad_clamp_fusion.1), kind=kCustom, calls=%fused_computation.2.clone | custom fusion | bytes 592128 | tf_op jit(solution)/shard_map/jit(_take)/gather | solution.py:153
  17.0 2.7 %gather_fusion = bf16[576,256]{1,0:T(8,128)(2,1)S(1)} fusion(bf16[129,256]{1,0:T(8,128)(2,1)S(1)} %concatenate.35, s32[1024]{0:T(1024)S(1)} %pad_clamp_fusion.1), kind=kCustom, calls=%fused_computation.clone | custom fusion | bytes 592128 | tf_op jit(solution)/shard_map/jit(_take)/gather | solution.py:153
  20.4 38.9 %all_to_all.21 = bf16[64,18,256]{2,1,0:T(8,128)(2,1)S(1)} all-to-all(bf16[64,18,256]{2,1,0:T(8,128)(2,1)S(1)} %pad_maximum_fusion.2), channel_id=1, replica_groups=mesh['dp'=64,'tensor'=8] {'dp'}, dimensions={0} | all-to-all | bytes 1179648 | tf_op jit(solution)/shard_map/all_to_all | solution.py:28
  59.7 0.8 pad_maximum_fusion.4
  60.8 0.7 concatenate.33
  61.6 39.5 %all-gather.5.cloned.1.call-done = bf16[128,9,2048]{2,0,1:T(8,128)(2,1)} async-done(((bf16[128,9,256]{2,0,1:T(8,128)(2,1)}), bf16[128,9,2048]{2,0,1:T(8,128)(2,1)}) %all-gather.5.cloned.1.call-update) | async-done | bytes 4718608 | tf_op jit(solution)/shard_map/all_gather | solution.py:41
  101.1 2.6 fusion.26
  103.7 0.4 copy-done.11
  104.2 0.8 fusion.29
  105.3 1.8 multiply_convert_fusion.2
  107.1 0.8 fusion
  107.9 3.5 %copy.52 = bf16[64,1,9,2048]{3,2,0,1:T(8,128)(2,1)} copy(bf16[64,1,9,2048]{3,0,2,1:T(8,128)(2,1)S(1)} %fusion) | data formatting | bytes 4718592 | tf_op jit(solution)/shard_map/convert_element_type | solution.py:104
  111.4 4.4 %reshape.172 = bf16[576,8,256]{2,1,0:T(8,128)(2,1)S(1)} reshape(bf16[64,1,9,2048]{3,2,0,1:T(8,128)(2,1)} %copy.52) | data formatting | bytes 4718592 | tf_op jit(solution)/shard_map/reshape | solution.py:166
  115.9 2.7 %fusion.1 = bf16[64,1,9,2048]{3,0,2,1:T(8,128)(2,1)S(1)} fusion(bf16[1,2048,176]{1,2,0:T(8,128)(2,1)S(1)} %copy-done.13, bf16[1,2048,176]{1,2,0:T(8,128)(2,1)} %param.25, bf16[64,1,9,176]{3,0,2,1:T(8,128)(2,1)} %get-tuple-element.17, bf16[64,1,9,176]{3,0,2,1:T(8,128)(2,1)} %get-tuple-element.16), kind=kOutput, calls=%fused_computation.9 | convolution fusion | flops 835346432 | bytes 4206592 | tf_op jit(solution)/shard_map/slcf,ldf->slcd/dot_general | solution.py:110
  118.6 3.5 %copy.53 = bf16[64,1,9,2048]{3,2,0,1:T(8,128)(2,1)} copy(bf16[64,1,9,2048]{3,0,2,1:T(8,128)(2,1)S(1)} %fusion.1) | data formatting | bytes 4718592 | tf_op jit(solution)/shard_map/convert_element_type | solution.py:113
  122.1 5.8 %reshape.175 = bf16[576,8,256]{2,1,0:T(8,128)(2,1)} reshape(bf16[64,1,9,2048]{3,2,0,1:T(8,128)(2,1)} %copy.53) | data formatting | bytes 4718592 | tf_op jit(solution)/shard_map/reshape | solution.py:167
  128.0 4.6 %pad_maximum_fusion = bf16[1152,8,256]{2,1,0:T(8,128)(2,1)S(1)} fusion(bf16[576,8,256]{2,1,0:T(8,128)(2,1)} %reshape.175, bf16[576,8,256]{2,1,0:T(8,128)(2,1)S(1)} %reshape.172), kind=kLoop, calls=%fused_computation.5 | loop fusion | flops 2359296 | bytes 9437184 | tf_op jit(solution)/shard_map/concatenate | solution.py:25
  132.6 3.2 %copy.54 = bf16[1152,8,256]{2,0,1:T(8,128)(2,1)} copy(bf16[1152,8,256]{2,1,0:T(8,128)(2,1)S(1)} %pad_maximum_fusion) | data formatting | bytes 9437184 | tf_op jit(solution)/shard_map/concatenate | solution.py:25
  135.7 5.1 %all-to-all-start.1 = ((bf16[1152,8,256]{2,0,1:T(8,128)(2,1)}), bf16[1152,8,256]{2,0,1:T(8,128)(2,1)}, u32[]{:S(2)}, u32[]{:S(2)}) async-start(bf16[1152,8,256]{2,0,1:T(8,128)(2,1)} %copy.54), calls=%async_computation.2 | async-start | bytes 9437184 | tf_op jit(solution)/shard_map/all_to_all | solution.py:28
  141.1 46.9 %all-gather.3.cloned.1.call-done = bf16[2048,1056]{1,0:T(8,128)(2,1)} async-done(((bf16[32,1056]{1,0:T(8,128)(2,1)}), bf16[2048,1056]{1,0:T(8,128)(2,1)}) %all-gather.3.cloned.1.call-update) | async-done | bytes 4325392 | tf_op jit(solution)/shard_map/all_gather | solution.py:12
  188.0 2.1 fusion.32
  190.2 2.7 %fusion.35 = f32[128,352]{0,1:T(8,128)S(1)} fusion(bf16[128,2048]{1,0:T(8,128)(2,1)S(1)} %copy-done.2, bf16[2048,1056]{1,0:T(8,128)(2,1)} %all-gather.3.cloned.1.call-done), kind=kOutput, calls=%fused_computation.39 | convolution fusion | flops 184549376 | bytes 2277376 | tf_op jit(solution)/shard_map/dot_general | solution.py:86
  192.9 1.1 fusion.38
  194.0 0.7 fusion.19
  194.7 1.0 fusion.3
  195.7 3.7 %slice_reduce_fusion.1 = (bf16[576,256]{1,0:T(8,128)(2,1)S(1)}, bf16[576,256]{1,0:T(8,128)(2,1)S(1)}) fusion(bf16[1152,8,256]{2,0,1:T(8,128)(2,1)} %all-to-all-done.1), kind=kLoop, calls=%fused_computation.14 | loop fusion | flops 2064384 | bytes 5308416 | tf_op jit(solution)/shard_map/reduce_sum | solution.py:169
  199.7 1.1 pad_maximum_fusion.3
  200.8 12.6 %all-to-all-start.2 = ((bf16[64,18,256]{2,1,0:T(8,128)(2,1)}), bf16[64,18,256]{2,1,0:T(8,128)(2,1)S(1)}, u32[]{:S(2)}, u32[]{:S(2)}) async-start(bf16[64,18,256]{2,1,0:T(8,128)(2,1)} %pad_maximum_fusion.3), calls=%async_computation.3 | async-start | bytes 1572864 | tf_op jit(solution)/shard_map/all_to_all | solution.py:28
  213.4 2.8 %multiply_convert_fusion = (bf16[128,2048]{1,0:T(8,128)(2,1)S(1)}, f32[128]{0:T(128)S(1)}) fusion(f32[128]{0:T(128)S(1)} %fusion.46, bf16[128,2048]{1,0:T(8,128)(2,1)} %param.17, bf16[2048,1056]{1,0:T(8,128)(2,1)} %all-gather.3.cloned.1.call-done, f32[128,352]{0,1:T(8,128)S(1)} %fusion.35, f32[128,352]{0,1:T(8,128)S(1)} %fusion.32), kind=kOutput, calls=%fused_computation.52 | convolution fusion | flops 186130304 | bytes 2982912 | tf_op jit(solution)/shard_map/dot_general | solution.py:89
  216.2 1.1 pad_maximum_fusion.1
  217.9 16.9 %all-to-all-done.2 = bf16[64,18,256]{2,1,0:T(8,128)(2,1)S(1)} async-done(((bf16[64,18,256]{2,1,0:T(8,128)(2,1)}), bf16[64,18,256]{2,1,0:T(8,128)(2,1)S(1)}, u32[]{:S(2)}, u32[]{:S(2)}) %all-to-all-start.2) | async-done | bytes 589856 | tf_op jit(solution)/shard_map/all_to_all | solution.py:28
  234.8 1.3 slice_convert_fusion.1
  236.1 1.3 reshape.185
  237.6 1.6 gather_fusion.3
  239.2 1.6 gather_fusion.2
  240.8 1.0 multiply_reduce_fusion.1
  241.8 0.6 broadcast_in_dim.23
  242.4 6.9 %all-to-all-start.3 = ((f32[8,1,640]{2,1,0:T(1,128)}), f32[8,1,640]{2,1,0:T(1,128)S(1)}, u32[]{:S(2)}, u32[]{:S(2)}) async-start(f32[8,1,640]{2,1,0:T(1,128)} %broadcast_in_dim.23), calls=%async_computation.4 | async-start | bytes 40960 | tf_op jit(solution)/shard_map/all_to_all | solution.py:46
  249.4 1.2 reshape.178
  250.7 3.3 %all-to-all-done.3 = f32[8,1,640]{2,1,0:T(1,128)S(1)} async-done(((f32[8,1,640]{2,1,0:T(1,128)}), f32[8,1,640]{2,1,0:T(1,128)S(1)}, u32[]{:S(2)}, u32[]{:S(2)}) %all-to-all-start.3) | async-done | bytes 20512 | tf_op jit(solution)/shard_map/all_to_all | solution.py:46
  254.5 0.7 multiply_reduce_fusion.2
  255.2 1.5 add_convert_fusion
  256.7 1.7 fusion.42
  (84 shorter events, 4.5 us)
Async XLA Ops:
  7.2 96.6 %copy-start = (bf16[1,176,2048]{2,1,0:T(8,128)(2,1)S(1)}, bf16[1,176,2048]{2,1,0:T(8,128)(2,1)}, u32[]{:S(2)}) copy-start(bf16[1,176,2048]{2,1,0:T(8,128)(2,1)} %param.27) | copy-start | bytes 2162692
  7.2 93.9 %all-gather.5.cloned.1.call-start = ((), (), s32[]{:S(2)}) async-start(), calls=%async_computation.7 | async-start | bytes 5308416 | tf_op jit(solution)/shard_map/all_gather | solution.py:41
  59.3 1.5 copy-start.5
  59.3 1.5 copy-start.6
  59.3 1.6 copy-start.7
  59.3 41.8 %copy-start.12 = (bf16[1,2048,176]{1,2,0:T(8,128)(2,1)S(1)}, bf16[1,2048,176]{1,2,0:T(8,128)(2,1)}, u32[]{:S(2)}) copy-start(bf16[1,2048,176]{1,2,0:T(8,128)(2,1)} %param.26) | copy-start | bytes 2162692
  60.6 127.4 %all-gather.3.cloned.1.call-start = ((), (), s32[]{:S(2)}) async-start(), calls=%async_computation.5 | async-start | bytes 4792320 | tf_op jit(solution)/shard_map/all_gather | solution.py:12
  101.1 3.0 %copy-start.11 = (bf16[128,9,2048]{2,0,1:T(8,128)(2,1)S(1)}, bf16[128,9,2048]{2,0,1:T(8,128)(2,1)}, u32[]{:S(2)}) copy-start(bf16[128,9,2048]{2,0,1:T(8,128)(2,1)} %all-gather.5.cloned.1.call-done) | copy-start | bytes 14155780
  104.2 1.1 copy-start.14
  111.4 4.4 %copy-start.13 = (bf16[1,2048,176]{1,2,0:T(8,128)(2,1)S(1)}, bf16[1,2048,176]{1,2,0:T(8,128)(2,1)}, u32[]{:S(2)}) copy-start(bf16[1,2048,176]{1,2,0:T(8,128)(2,1)} %param.26) | copy-start | bytes 2162692
  135.7 5.1 %copy-start.10 = (bf16[2048]{0:T(1024)(128)(2,1)S(1)}, bf16[2048]{0:T(1024)(128)(2,1)}, u32[]{:S(2)}) copy-start(bf16[2048]{0:T(1024)(128)(2,1)} %param.21) | copy-start | bytes 12292
  135.7 5.1 %copy-start.2 = (bf16[128,2048]{1,0:T(8,128)(2,1)S(1)}, bf16[128,2048]{1,0:T(8,128)(2,1)}, u32[]{:S(2)}) copy-start(bf16[128,2048]{1,0:T(8,128)(2,1)} %param.16) | copy-start | bytes 1572868
  135.7 59.9 %all-to-all-start.1 = ((bf16[1152,8,256]{2,0,1:T(8,128)(2,1)}), bf16[1152,8,256]{2,0,1:T(8,128)(2,1)}, u32[]{:S(2)}, u32[]{:S(2)}) async-start(bf16[1152,8,256]{2,0,1:T(8,128)(2,1)} %copy.54), calls=%async_computation.2 | async-start | bytes 9437184 | tf_op jit(solution)/shard_map/all_to_all | solution.py:28
  141.1 51.7 %copy-start.9 = (bf16[128,2048]{1,0:T(8,128)(2,1)S(1)}, bf16[128,2048]{1,0:T(8,128)(2,1)}, u32[]{:S(2)}) copy-start(bf16[128,2048]{1,0:T(8,128)(2,1)} %param.17) | copy-start | bytes 1572868
  188.0 4.9 %copy-start.3 = (bf16[2048,1056]{1,0:T(8,128)(2,1)S(1)}, bf16[2048,1056]{1,0:T(8,128)(2,1)}, u32[]{:S(2)}) copy-start(bf16[2048,1056]{1,0:T(8,128)(2,1)} %all-gather.3.cloned.1.call-done) | copy-start | bytes 12976132
  200.8 34.0 %all-to-all-start.2 = ((bf16[64,18,256]{2,1,0:T(8,128)(2,1)}), bf16[64,18,256]{2,1,0:T(8,128)(2,1)S(1)}, u32[]{:S(2)}, u32[]{:S(2)}) async-start(bf16[64,18,256]{2,1,0:T(8,128)(2,1)} %pad_maximum_fusion.3), calls=%async_computation.3 | async-start | bytes 1572864 | tf_op jit(solution)/shard_map/all_to_all | solution.py:28
  213.4 41.8 %reduce-scatter.2.cloned.1.call-start = ((), (), s32[]{:S(2)}) async-start(), calls=%async_computation.6 | async-start | bytes 1179648 | tf_op jit(solution)/shard_map/reduce_scatter | solution.py:69
  216.2 1.4 copy-start.4
  240.8 13.5 %copy-start.8 = (s32[128,4]{0,1:T(4,128)S(1)}, s32[128,4]{0,1:T(4,128)}, u32[]{:S(2)}) copy-start(s32[128,4]{0,1:T(4,128)} %param.18) | copy-start | bytes 6148
  240.8 17.7 %copy-start.1 = (bf16[1,176,2048]{2,1,0:T(8,128)(2,1)S(1)}, bf16[1,176,2048]{2,1,0:T(8,128)(2,1)}, u32[]{:S(2)}) copy-start(bf16[1,176,2048]{2,1,0:T(8,128)(2,1)} %param.27) | copy-start | bytes 2162692
  242.4 11.6 %all-to-all-start.3 = ((f32[8,1,640]{2,1,0:T(1,128)}), f32[8,1,640]{2,1,0:T(1,128)S(1)}, u32[]{:S(2)}, u32[]{:S(2)}) async-start(f32[8,1,640]{2,1,0:T(1,128)} %broadcast_in_dim.23), calls=%async_computation.4 | async-start | bytes 40960 | tf_op jit(solution)/shard_map/all_to_all | solution.py:46
Sparse Core Ops, SparseCore 0:
  60.7 40.3 all-gather.4
  104.1 83.8 all-gather.2
  217.4 36.9 reduce-scatter.1
where the time goes:
time: 266 us; the launch traced here: 265 us
  waiting for transfers between devices  107 us (40%)
  local copies, waits for them, and re-layouts  40.2 us (15%)
  blocking collectives  38.9 us (15%)
  starting transfers between devices  24.9 us (9%)
  matrix products  21.4 us (8%)
  other arithmetic  18.6 us (7%)
  between operations  14.3 us (5%)
    all_gather x1, waiting for transfers between devices, turned_gather(): result, at, outs = (lax.all_gather(both, axis, axis=0, tiled=True), 0, [])  46.9 us
    all_gather x1, waiting for transfers between devices, in_one_piece_2(): lax.all_gather(both, axis, axis=dim, tiled=True)  39.5 us
    all_to_all x1, blocking collectives, in_one_piece(): lax.all_to_all(both, axis, split_axis=split_dim, concat_axis=concat_dim,...  38.9 us
    all_to_all x2, starting transfers between devices, in_one_piece(): lax.all_to_all(both, axis, split_axis=split_dim, concat_axis=concat_dim,...  17.7 us
    all_to_all x2, waiting for transfers between devices, in_one_piece(): lax.all_to_all(both, axis, split_axis=split_dim, concat_axis=concat_dim,...  16.9 us
    all_to_all x1, starting transfers between devices, copy_for_each(): lax.all_to_all(jnp.broadcast_to(x[None], (peers, *x.shape)), axis, 0, 0,...  6.92 us
    concatenate x3, other arithmetic, in_one_piece(): both = jnp.concatenate(arrays, axis=along)  5.99 us
    reshape x1, local copies, waits for them, and re-layouts, run_routed(): split_back = backward.reshape(buffer_rows, tensor_size, col_width)  5.82 us
  transfers between devices with their start and end apart: 6, of which 4 were waited for; matrix products, arithmetic and copies ran while one was open for 21% of the time, Pallas kernels for 0%

commit v1 on v0

--- a/solution.py
+++ b/solution.py
@@ -9,7 +9,13 @@
 def turned_gather(arrays, axis, dims):
     turned = [jnp.moveaxis(a, dim, 0) for a, dim in zip(arrays, dims)]
     both = jnp.concatenate([t.reshape(len(t), -1) for t in turned], axis=1)
-    result, at, outs = (lax.all_gather(both, axis, axis=0, tiled=True), 0, [])
+    result, at, outs = (
+        jnp.concatenate(
+            lax.all_to_all(jnp.stack([both] * lax.axis_size(axis)), axis, 0, 0), axis=0
+        ),
+        0,
+        [],
+    )
     for t, dim in zip(turned, dims):
         share = result[:, at : at + t[0].size].reshape(-1, *t.shape[1:])
         outs.append(jnp.moveaxis(share, 0, dim))

time: 266 us -> 347 us (1.30)
  starting transfers between devices: 24.9 us -> 62.6 us
  waiting for transfers between devices: 107 us -> 143 us
  matrix products: 21.4 us -> 25.8 us
    all_to_all x0 -> x1, waiting for transfers between devices: none -> 51.3 us  [turned_gather(): lax.all_to_all(jnp.stack([both] * lax.axis_size(axis)), axis, 0, 0)]
    all_gather x1 -> x0, waiting for transfers between devices: 46.9 us -> none  [turned_gather(): result, at, outs = (lax.all_gather(both, axis, axis=0, tiled=True), 0, [])]
    all_to_all x2, waiting for transfers between devices: 16.9 us -> 58.9 us  [in_one_piece(): lax.all_to_all(both, axis, split_axis=split_dim, concat_axis=concat_dim,...]
    all_to_all x2, starting transfers between devices: 17.7 us -> 47.5 us  [in_one_piece(): lax.all_to_all(both, axis, split_axis=split_dim, concat_axis=concat_dim,...]
    all_gather x1, waiting for transfers between devices: 39.5 us -> 29.7 us  [in_one_piece_2(): lax.all_gather(both, axis, axis=dim, tiled=True)]
    all_to_all x0 -> x1, starting transfers between devices: none -> 8.16 us  [turned_gather(): lax.all_to_all(jnp.stack([both] * lax.axis_size(axis)), axis, 0, 0)]
    dot_general x3, matrix products: 2.78 us -> 7.36 us  [contract_last(): lax.dot_general(left, right, (((1,), (1,)), ((), ())), preferred_element_...]
  transfers between devices with their start and end apart: 6 -> 6, of which waited for: 4 -> 5; matrix products, arithmetic and copies ran while one was open for 21% -> 18% of each run, Pallas kernels for 0% -> 0%
where the time goes in v1:
time: 347 us; the launch traced here: 346 us
  waiting for transfers between devices  143 us (41%)
  starting transfers between devices  62.6 us (18%)
  local copies, waits for them, and re-layouts  42.2 us (12%)
  blocking collectives  38.9 us (11%)
  matrix products  25.8 us (7%)
  other arithmetic  18.6 us (5%)
  between operations  14.6 us (4%)
    all_to_all x2, waiting for transfers between devices, in_one_piece(): lax.all_to_all(both, axis, split_axis=split_dim, concat_axis=concat_dim,...  58.9 us
    all_to_all x1, waiting for transfers between devices, turned_gather(): lax.all_to_all(jnp.stack([both] * lax.axis_size(axis)), axis, 0, 0)  51.3 us
    all_to_all x2, starting transfers between devices, in_one_piece(): lax.all_to_all(both, axis, split_axis=split_dim, concat_axis=concat_dim,...  47.5 us
    all_to_all x1, blocking collectives, in_one_piece(): lax.all_to_all(both, axis, split_axis=split_dim, concat_axis=concat_dim,...  38.9 us
    all_gather x1, waiting for transfers between devices, in_one_piece_2(): lax.all_gather(both, axis, axis=dim, tiled=True)  29.7 us
    all_to_all x1, starting transfers between devices, turned_gather(): lax.all_to_all(jnp.stack([both] * lax.axis_size(axis)), axis, 0, 0)  8.16 us
    dot_general x3, matrix products, contract_last(): lax.dot_general(left, right, (((1,), (1,)), ((), ())), preferred_element_...  7.36 us
  transfers between devices with their start and end apart: 6, of which 5 were waited for; matrix products, arithmetic and copies ran while one was open for 18% of the time, Pallas kernels for 0%

profile of v1, /device:TPU:1, one launch (start us, length us, event | category | flops | bytes accessed | tf_op | source)
XLA Modules:
  0.0 346.0 jit_solution(279288285996142847)
XLA Ops:
  7.2 0.8 copy.47
  8.3 1.2 reduce-window.6
  10.1 0.8 select_reduce_fusion
  10.8 2.4 scatter_custom_fusion
  13.3 0.9 constant_dynamic-slice_fusion
  14.3 2.7 gather_fusion.1
  17.0 2.7 gather_fusion
  20.4 38.9 %all_to_all.26 = bf16[64,18,256]{2,1,0:T(8,128)(2,1)S(1)} all-to-all(bf16[64,18,256]{2,1,0:T(8,128)(2,1)S(1)} %pad_maximum_fusion.2), channel_id=1, replica_groups=mesh['dp'=64,'tensor'=8] {'dp'}, dimensions={0} | all-to-all | bytes 1179648 | tf_op jit(solution)/shard_map/all_to_all | solution.py:34
  59.7 0.8 pad_maximum_fusion.4
  60.7 2.5 stack.2
  63.2 8.2 %all-to-all-start = ((bf16[64,32,1056]{2,1,0:T(8,128)(2,1)}), bf16[64,32,1056]{2,1,0:T(8,128)(2,1)}, u32[]{:S(2)}, u32[]{:S(2)}) async-start(bf16[64,32,1056]{2,1,0:T(8,128)(2,1)} %stack.2), calls=%async_computation | async-start | bytes 9437184 | tf_op jit(solution)/shard_map/all_to_all | solution.py:14
  71.4 29.7 %all-gather.2.cloned.1.call-done = bf16[128,9,2048]{2,0,1:T(8,128)(2,1)} async-done(((bf16[128,9,256]{2,0,1:T(8,128)(2,1)}), bf16[128,9,2048]{2,0,1:T(8,128)(2,1)}) %all-gather.2.cloned.1.call-update) | async-done | bytes 4718608 | tf_op jit(solution)/shard_map/all_gather | solution.py:47
  101.1 2.6 fusion.26
  104.2 0.8 fusion.29
  105.3 1.8 multiply_convert_fusion.2
  107.0 0.8 fusion
  107.8 3.6 %copy.52 = bf16[64,1,9,2048]{3,2,0,1:T(8,128)(2,1)} copy(bf16[64,1,9,2048]{3,0,2,1:T(8,128)(2,1)S(1)} %fusion) | data formatting | bytes 4718592 | tf_op jit(solution)/shard_map/convert_element_type | solution.py:110
  111.4 4.4 %reshape.178 = bf16[576,8,256]{2,1,0:T(8,128)(2,1)S(1)} reshape(bf16[64,1,9,2048]{3,2,0,1:T(8,128)(2,1)} %copy.52) | data formatting | bytes 4718592 | tf_op jit(solution)/shard_map/reshape | solution.py:172
  115.9 2.7 fusion.1
  118.6 3.6 %copy.53 = bf16[64,1,9,2048]{3,2,0,1:T(8,128)(2,1)} copy(bf16[64,1,9,2048]{3,0,2,1:T(8,128)(2,1)S(1)} %fusion.1) | data formatting | bytes 4718592 | tf_op jit(solution)/shard_map/convert_element_type | solution.py:119
  122.1 5.8 %reshape.181 = bf16[576,8,256]{2,1,0:T(8,128)(2,1)} reshape(bf16[64,1,9,2048]{3,2,0,1:T(8,128)(2,1)} %copy.53) | data formatting | bytes 4718592 | tf_op jit(solution)/shard_map/reshape | solution.py:173
  128.0 4.6 %pad_maximum_fusion = bf16[1152,8,256]{2,1,0:T(8,128)(2,1)S(1)} fusion(bf16[576,8,256]{2,1,0:T(8,128)(2,1)} %reshape.181, bf16[576,8,256]{2,1,0:T(8,128)(2,1)S(1)} %reshape.178), kind=kLoop, calls=%fused_computation.5 | loop fusion | flops 2359296 | bytes 9437184 | tf_op jit(solution)/shard_map/concatenate | solution.py:31
  132.6 3.2 copy.54
  135.8 51.3 %all-to-all-done = bf16[64,32,1056]{2,1,0:T(8,128)(2,1)} async-done(((bf16[64,32,1056]{2,1,0:T(8,128)(2,1)}), bf16[64,32,1056]{2,1,0:T(8,128)(2,1)}, u32[]{:S(2)}, u32[]{:S(2)}) %all-to-all-start) | async-done | bytes 4325408 | tf_op jit(solution)/shard_map/all_to_all | solution.py:14
  187.1 8.5 %all-to-all-start.2 = ((bf16[1152,8,256]{2,0,1:T(8,128)(2,1)}), bf16[1152,8,256]{2,0,1:T(8,128)(2,1)}, u32[]{:S(2)}, u32[]{:S(2)}) async-start(bf16[1152,8,256]{2,0,1:T(8,128)(2,1)} %copy.54), calls=%async_computation.3 | async-start | bytes 9437184 | tf_op jit(solution)/shard_map/all_to_all | solution.py:34
  195.9 2.1 fusion.32
  198.0 2.7 fusion.35
  200.7 2.7 fusion.38
  203.3 2.1 fusion.19
  205.4 2.6 fusion.3
  208.0 42.0 %all-to-all-done.2 = bf16[1152,8,256]{2,0,1:T(8,128)(2,1)} async-done(((bf16[1152,8,256]{2,0,1:T(8,128)(2,1)}), bf16[1152,8,256]{2,0,1:T(8,128)(2,1)}, u32[]{:S(2)}, u32[]{:S(2)}) %all-to-all-start.2) | async-done | bytes 4718624 | tf_op jit(solution)/shard_map/all_to_all | solution.py:34
  250.0 3.7 %slice_reduce_fusion.1 = (bf16[576,256]{1,0:T(8,128)(2,1)S(1)}, bf16[576,256]{1,0:T(8,128)(2,1)S(1)}) fusion(bf16[1152,8,256]{2,0,1:T(8,128)(2,1)} %all-to-all-done.2), kind=kLoop, calls=%fused_computation.14 | loop fusion | flops 2064384 | bytes 5308416 | tf_op jit(solution)/shard_map/reduce_sum | solution.py:175
  254.0 1.1 pad_maximum_fusion.3
  255.1 38.9 %all-to-all-start.3 = ((bf16[64,18,256]{2,1,0:T(8,128)(2,1)}), bf16[64,18,256]{2,1,0:T(8,128)(2,1)S(1)}, u32[]{:S(2)}, u32[]{:S(2)}) async-start(bf16[64,18,256]{2,1,0:T(8,128)(2,1)} %pad_maximum_fusion.3), calls=%async_computation.4 | async-start | bytes 1572864 | tf_op jit(solution)/shard_map/all_to_all | solution.py:34
  294.1 2.8 multiply_convert_fusion
  296.9 1.1 pad_maximum_fusion.1
  298.6 16.9 %all-to-all-done.3 = bf16[64,18,256]{2,1,0:T(8,128)(2,1)S(1)} async-done(((bf16[64,18,256]{2,1,0:T(8,128)(2,1)}), bf16[64,18,256]{2,1,0:T(8,128)(2,1)S(1)}, u32[]{:S(2)}, u32[]{:S(2)}) %all-to-all-start.3) | async-done | bytes 589856 | tf_op jit(solution)/shard_map/all_to_all | solution.py:34
  315.5 1.3 slice_convert_fusion.1
  316.8 1.3 reshape.191
  318.2 1.6 gather_fusion.3
  319.8 1.6 gather_fusion.2
  321.4 1.0 multiply_reduce_fusion.1
  323.0 6.9 %all-to-all-start.4 = ((f32[8,1,640]{2,1,0:T(1,128)}), f32[8,1,640]{2,1,0:T(1,128)S(1)}, u32[]{:S(2)}, u32[]{:S(2)}) async-start(f32[8,1,640]{2,1,0:T(1,128)} %broadcast_in_dim.23), calls=%async_computation.5 | async-start | bytes 40960 | tf_op jit(solution)/shard_map/all_to_all | solution.py:52
  330.0 1.2 reshape.184
  331.4 3.3 all-to-all-done.4
  335.2 0.7 multiply_reduce_fusion.2
  335.9 1.5 add_convert_fusion
  337.4 1.7 fusion.42
  (82 shorter events, 5.4 us)
Async XLA Ops:
  7.2 96.6 %copy-start = (bf16[1,176,2048]{2,1,0:T(8,128)(2,1)S(1)}, bf16[1,176,2048]{2,1,0:T(8,128)(2,1)}, u32[]{:S(2)}) copy-start(bf16[1,176,2048]{2,1,0:T(8,128)(2,1)} %param.27) | copy-start | bytes 2162692
  7.2 93.9 %all-gather.2.cloned.1.call-start = ((), (), s32[]{:S(2)}) async-start(), calls=%async_computation.7 | async-start | bytes 5308416 | tf_op jit(solution)/shard_map/all_gather | solution.py:47
  59.3 1.3 copy-start.4
  59.3 1.3 copy-start.5
  59.3 1.3 copy-start.6
  63.2 37.9 %copy-start.11 = (bf16[1,2048,176]{1,2,0:T(8,128)(2,1)S(1)}, bf16[1,2048,176]{1,2,0:T(8,128)(2,1)}, u32[]{:S(2)}) copy-start(bf16[1,2048,176]{1,2,0:T(8,128)(2,1)} %param.26) | copy-start | bytes 2162692
  63.2 123.8 %all-to-all-start = ((bf16[64,32,1056]{2,1,0:T(8,128)(2,1)}), bf16[64,32,1056]{2,1,0:T(8,128)(2,1)}, u32[]{:S(2)}, u32[]{:S(2)}) async-start(bf16[64,32,1056]{2,1,0:T(8,128)(2,1)} %stack.2), calls=%async_computation | async-start | bytes 9437184 | tf_op jit(solution)/shard_map/all_to_all | solution.py:14
  101.1 3.0 copy-start.10
  104.2 1.1 copy-start.13
  111.4 4.4 %copy-start.12 = (bf16[1,2048,176]{1,2,0:T(8,128)(2,1)S(1)}, bf16[1,2048,176]{1,2,0:T(8,128)(2,1)}, u32[]{:S(2)}) copy-start(bf16[1,2048,176]{1,2,0:T(8,128)(2,1)} %param.26) | copy-start | bytes 2162692
  135.8 59.8 %copy-start.9 = (bf16[2048]{0:T(1024)(128)(2,1)S(1)}, bf16[2048]{0:T(1024)(128)(2,1)}, u32[]{:S(2)}) copy-start(bf16[2048]{0:T(1024)(128)(2,1)} %param.21) | copy-start | bytes 12292
  135.8 59.9 %copy-start.2 = (bf16[128,2048]{1,0:T(8,128)(2,1)S(1)}, bf16[128,2048]{1,0:T(8,128)(2,1)}, u32[]{:S(2)}) copy-start(bf16[128,2048]{1,0:T(8,128)(2,1)} %param.16) | copy-start | bytes 1572868
  187.1 63.0 %all-to-all-start.2 = ((bf16[1152,8,256]{2,0,1:T(8,128)(2,1)}), bf16[1152,8,256]{2,0,1:T(8,128)(2,1)}, u32[]{:S(2)}, u32[]{:S(2)}) async-start(bf16[1152,8,256]{2,0,1:T(8,128)(2,1)} %copy.54), calls=%async_computation.3 | async-start | bytes 9437184 | tf_op jit(solution)/shard_map/all_to_all | solution.py:34
  195.9 4.8 %copy-start.8 = (bf16[128,2048]{1,0:T(8,128)(2,1)S(1)}, bf16[128,2048]{1,0:T(8,128)(2,1)}, u32[]{:S(2)}) copy-start(bf16[128,2048]{1,0:T(8,128)(2,1)} %param.17) | copy-start | bytes 1572868
  255.1 60.4 %all-to-all-start.3 = ((bf16[64,18,256]{2,1,0:T(8,128)(2,1)}), bf16[64,18,256]{2,1,0:T(8,128)(2,1)S(1)}, u32[]{:S(2)}, u32[]{:S(2)}) async-start(bf16[64,18,256]{2,1,0:T(8,128)(2,1)} %pad_maximum_fusion.3), calls=%async_computation.4 | async-start | bytes 1572864 | tf_op jit(solution)/shard_map/all_to_all | solution.py:34
  294.0 41.9 %reduce-scatter.2.cloned.1.call-start = ((), (), s32[]{:S(2)}) async-start(), calls=%async_computation.6 | async-start | bytes 1179648 | tf_op jit(solution)/shard_map/reduce_scatter | solution.py:75
  296.9 1.4 copy-start.3
  321.4 13.5 %copy-start.7 = (s32[128,4]{0,1:T(4,128)S(1)}, s32[128,4]{0,1:T(4,128)}, u32[]{:S(2)}) copy-start(s32[128,4]{0,1:T(4,128)} %param.18) | copy-start | bytes 6148
  321.4 17.7 %copy-start.1 = (bf16[1,176,2048]{2,1,0:T(8,128)(2,1)S(1)}, bf16[1,176,2048]{2,1,0:T(8,128)(2,1)}, u32[]{:S(2)}) copy-start(bf16[1,176,2048]{2,1,0:T(8,128)(2,1)} %param.27) | copy-start | bytes 2162692
  323.0 11.6 %all-to-all-start.4 = ((f32[8,1,640]{2,1,0:T(1,128)}), f32[8,1,640]{2,1,0:T(1,128)S(1)}, u32[]{:S(2)}, u32[]{:S(2)}) async-start(f32[8,1,640]{2,1,0:T(1,128)} %broadcast_in_dim.23), calls=%async_computation.5 | async-start | bytes 40960 | tf_op jit(solution)/shard_map/all_to_all | solution.py:52
Sparse Core Ops, SparseCore 0:
  60.7 40.3 all-gather.1
  298.1 35.6 reduce-scatter.1
